TPU v7x, 8 devices: a whole 2x2x1 slice. The times are simulated.
8 devices in a mesh: dp: 2 (over z, y), row: 2 (over x), fsdp: 2 (over core).
Axes of the slice: x: 2, y: 2, z: 1, core: 2. Of those that a mesh axis runs over, the one named last changes fastest.
Arguments:
- x_saved: bfloat16 [2, 16384, 896], P(None, ('dp', 'row', 'fsdp'))
- dy_out: bfloat16 [2, 16384, 896], P(None, ('dp', 'row', 'fsdp'))
- w_gate: bfloat16 [896, 4864], P(None, ('row', 'fsdp'))
- w_up: bfloat16 [896, 4864], P(None, ('row', 'fsdp'))
- w_down: bfloat16 [4864, 896], P(('row', 'fsdp'))
- g_next: float32 [8, 3, 896, 4864], P(('dp', 'row', 'fsdp'))
Outputs:
- output 1: bfloat16 [2, 16384, 896], P(None, ('dp', 'row', 'fsdp'))
- output 2: float32 [3, 896, 4864], P(None, None, ('row', 'fsdp'))
- output 3: float32 [8, 3, 896, 4864], P(('dp', 'row', 'fsdp'))
All inputs are finite; a program needn't handle non-finite values.
Results may differ from a plain program's by a relative error of at most 0.00911364.
Values are sent between devices in bfloat16 or wider.
A program may use at most 1 GiB of HBM per device.

v0:
```python
import jax
import jax.numpy as jnp
from jax import lax
from jax.sharding import PartitionSpec as P

TOK_AXES = ("dp", "row", "fsdp")
GROUP_AXES = ("row", "fsdp")


def mlp_backward(x_flat, dy_flat, w_gate, w_up, w_down):
    pre_gate = jnp.dot(x_flat, w_gate, preferred_element_type=jnp.float32)
    pre_up = jnp.dot(x_flat, w_up, preferred_element_type=jnp.float32)
    sig_gate = jax.nn.sigmoid(pre_gate)
    act_gate = pre_gate * sig_gate
    hidden = (act_gate * pre_up).astype(jnp.bfloat16)
    d_hidden = jnp.einsum("td,fd->tf", dy_flat, w_down, preferred_element_type=jnp.float32)
    d_gate = (d_hidden * pre_up * sig_gate * (1.0 + pre_gate * (1.0 - sig_gate))).astype(jnp.bfloat16)
    d_up = (d_hidden * act_gate).astype(jnp.bfloat16)
    dx_flat = (jnp.einsum("tf,df->td", d_gate, w_gate, preferred_element_type=jnp.float32) + jnp.einsum("tf,df->td", d_up, w_up, preferred_element_type=jnp.float32)).astype(jnp.bfloat16)
    grad_layer = jnp.stack([
        jnp.einsum("td,tf->df", x_flat, d_gate, preferred_element_type=jnp.float32),
        jnp.einsum("td,tf->df", x_flat, d_up, preferred_element_type=jnp.float32),
        jnp.einsum("td,tf->df", dy_flat, hidden, preferred_element_type=jnp.float32),
    ])
    return dx_flat, grad_layer


def solution(mesh):
    def local_step(x_dev, dy_dev, gate_shard, up_shard, down_shard, g_dev):
        w_gate = lax.all_gather(gate_shard, GROUP_AXES, axis=1, tiled=True)
        w_up = lax.all_gather(up_shard, GROUP_AXES, axis=1, tiled=True)
        w_down = lax.all_gather(down_shard, GROUP_AXES, axis=0, tiled=True)
        g_shard = lax.psum_scatter(g_dev[0].astype(jnp.bfloat16), GROUP_AXES, scatter_dimension=2, tiled=True)
        grad_next = lax.psum(g_shard.astype(jnp.float32), "dp")
        micro_count, tok_dev, d_model = x_dev.shape
        dx_flat, grad_layer = mlp_backward(x_dev.reshape(micro_count * tok_dev, d_model), dy_dev.reshape(micro_count * tok_dev, d_model), w_gate, w_up, w_down)
        return dx_flat.reshape(micro_count, tok_dev, d_model), grad_next, grad_layer[None]

    in_specs = (P(None, TOK_AXES, None), P(None, TOK_AXES, None), P(None, GROUP_AXES), P(None, GROUP_AXES), P(GROUP_AXES, None), P(TOK_AXES, None, None, None))
    out_specs = (P(None, TOK_AXES, None), P(None, None, GROUP_AXES), P(TOK_AXES, None, None, None))
    return jax.shard_map(local_step, mesh=mesh, in_specs=in_specs, out_specs=out_specs, check_vma=False)
```

profile of v0, /device:TPU:0, one launch (start us, length us, event | category | flops | bytes accessed | tf_op | source)
XLA Modules:
  0.0 947.6 jit_solution(14585465891965055997)
XLA Ops:
  7.2 0.0 all-gather.8.cloned.1.call-start
  7.2 0.7 all-gather.8.cloned.1.call-update
  7.9 0.0 all-gather.6.cloned.1.call-start
  7.9 0.7 all-gather.6.cloned.1.call-update
  8.6 0.0 all-gather.4.cloned.1.call-start
  8.7 0.7 all-gather.4.cloned.1.call-update
  9.4 0.0 reduce-scatter.2.cloned.1.call-start
  9.4 41.1 %copy.9 = bf16[1,3,896,4864]{2,3,1,0:T(8,128)(2,1)} copy(f32[1,3,896,4864]{3,2,1,0:T(8,128)} %param.11) | data formatting | bytes 78446592 | tf_op args[5]
  50.5 0.0 reduce-scatter.2.cloned.1.call-update
  50.5 19.4 %all-gather.8.cloned.1.call-done = bf16[896,4864]{0,1:T(8,128)(2,1)} async-done(((bf16[896,1216]{0,1:T(8,128)(2,1)}), bf16[896,4864]{0,1:T(8,128)(2,1)}) %all-gather.8.cloned.1.call-update) | async-done | bytes 8716304 | tf_op jit(solution)/shard_map/all_gather | solution.py:30
  70.0 50.3 %fusion.6 = f32[4096,4864]{1,0:T(8,128)} fusion(bf16[4096,896]{1,0:T(8,128)(2,1)} %bitcast.40, bf16[896,4864]{0,1:T(8,128)(2,1)} %all-gather.8.cloned.1.call-done), kind=kOutput, calls=%fused_computation.14 | convolution fusion | flops 35701915648 | bytes 95748096 | tf_op jit(solution)/shard_map/dot_general | solution.py:11
  120.3 8.8 all-gather.6.cloned.1.call-done
  129.1 50.3 %fusion.5 = f32[4096,4864]{1,0:T(8,128)} fusion(bf16[4096,896]{1,0:T(8,128)(2,1)} %bitcast.41, bf16[896,4864]{0,1:T(8,128)(2,1)} %all-gather.6.cloned.1.call-done), kind=kOutput, calls=%fused_computation.13 | convolution fusion | flops 35701915648 | bytes 95748096 | tf_op jit(solution)/shard_map/dot_general | solution.py:12
  179.5 8.8 all-gather.4.cloned.1.call-done
  188.3 96.9 %multiply_convert_fusion.1 = (bf16[4096,4864]{1,0:T(8,128)(2,1)}, bf16[4096,4864]{1,0:T(8,128)(2,1)}) fusion(f32[4096,4864]{1,0:T(8,128)} %fusion.6, f32[4096,4864]{1,0:T(8,128)} %fusion.5, bf16[4096,896]{1,0:T(8,128)(2,1)} %bitcast.44, bf16[4864,896]{1,0:T(8,128)(2,1)} %all-gather.4.cloned.1.call-done), kind=kOutput, calls=%fused_computation.1 | convolution fusion | flops 35960913920 | bytes 255131648 | tf_op jit(solution)/shard_map/td,fd->tf/dot_general | solution.py:16
  285.2 52.8 %convolution_bitcast_fusion = f32[1,896,4864]{1,2,0:T(8,128)} fusion(bf16[4096,4864]{1,0:T(8,128)(2,1)} %get-tuple-element.6, bf16[4096,896]{1,0:T(8,128)(2,1)} %bitcast.42), kind=kOutput, calls=%fused_computation.9 | convolution fusion | flops 35701915648 | bytes 64618496 | tf_op jit(solution)/shard_map/td,tf->df/dot_general | solution.py:22
  338.0 53.4 %convolution_bitcast_fusion.1 = f32[1,896,4864]{1,2,0:T(8,128)} fusion(bf16[4096,4864]{1,0:T(8,128)(2,1)} %get-tuple-element.7, bf16[4096,896]{1,0:T(8,128)(2,1)} %bitcast.43), kind=kOutput, calls=%fused_computation.10 | convolution fusion | flops 35701915648 | bytes 64618496 | tf_op jit(solution)/shard_map/td,tf->df/dot_general | solution.py:21
  391.4 64.9 %fusion.3 = f32[1,896,4864]{1,2,0:T(8,128)} fusion(bf16[4096,896]{1,0:T(8,128)(2,1)} %bitcast.45, f32[4096,4864]{1,0:T(8,128)} %fusion.5, f32[4096,4864]{1,0:T(8,128)} %fusion.6), kind=kOutput, calls=%fused_computation.11 | convolution fusion | flops 35821453312 | bytes 184156160 | tf_op jit(solution)/shard_map/td,tf->df/dot_general | solution.py:23
  456.3 34.6 %maximum_bitcast_fusion = f32[1,3,896,4864]{2,3,1,0:T(8,128)} fusion(f32[1,896,4864]{1,2,0:T(8,128)} %fusion.3, f32[1,896,4864]{1,2,0:T(8,128)} %convolution_bitcast_fusion, f32[1,896,4864]{1,2,0:T(8,128)} %convolution_bitcast_fusion.1), kind=kLoop, calls=%fused_computation.5 | loop fusion | flops 26148864 | bytes 104595456 | tf_op jit(solution)/shard_map/broadcast_in_dim | solution.py:37
  490.8 0.0 slice-start
  490.8 52.9 %copy.10 = f32[1,3,896,4864]{3,2,1,0:T(8,128)} copy(f32[1,3,896,4864]{2,3,1,0:T(8,128)} %maximum_bitcast_fusion) | data formatting | bytes 104595456
  543.7 0.0 slice-start.1
  543.7 0.0 slice-start.2
  543.7 50.0 %fusion.7 = f32[4096,896]{1,0:T(8,128)} fusion(bf16[4096,4864]{1,0:T(8,128)(2,1)} %get-tuple-element.7, bf16[896,4864]{0,1:T(8,128)(2,1)} %all-gather.8.cloned.1.call-done), kind=kOutput, calls=%fused_computation.15 | convolution fusion | flops 35701915648 | bytes 63242240 | tf_op jit(solution)/shard_map/tf,df->td/dot_general | solution.py:19
  593.7 0.0 slice-done
  593.7 0.0 slice-done.1
  593.7 0.0 slice-done.2
  593.7 46.8 %add_convert_fusion = bf16[4096,896]{1,0:T(8,128)(2,1)} fusion(f32[4096,896]{1,0:T(8,128)} %fusion.7, bf16[4096,4864]{1,0:T(8,128)(2,1)} %get-tuple-element.6, bf16[896,4864]{0,1:T(8,128)(2,1)S(1)} %bitcast.39), kind=kOutput, calls=%fused_computation.8 | convolution fusion | flops 35709255680 | bytes 70582272 | tf_op jit(solution)/shard_map/tf,df->td/dot_general | solution.py:19
  640.6 0.0 reduce-scatter.2.cloned.1.call-done
  640.6 300.3 %all-reduce.1 = f32[3,896,1216]{1,2,0:T(8,128)} all-reduce(bf16[3,896,1216]{1,2,0:T(8,128)(2,1)} %reduce-scatter.2.cloned.1.call-done), channel_id=1, replica_groups=mesh['dp'=2,'row'=2,'fsdp'=2] {'dp'}, use_global_device_ids=true, to_apply=%region_1.0 | all-reduce | flops 3268608 | bytes 19611648 | tf_op jit(solution)/shard_map/psum | solution.py:34
  (1 shorter events, 0.0 us)
Async XLA Ops:
  7.2 62.8 %all-gather.8.cloned.1.call-start = ((), (), s32[]{:S(2)}) async-start(), calls=%async_computation.3 | async-start | bytes 10895360 | tf_op jit(solution)/shard_map/all_gather | solution.py:30
  7.9 121.2 %all-gather.6.cloned.1.call-start = ((), (), s32[]{:S(2)}) async-start(), calls=%async_computation.2 | async-start | bytes 10895360 | tf_op jit(solution)/shard_map/all_gather | solution.py:31
  8.6 179.7 %all-gather.4.cloned.1.call-start = ((), (), s32[]{:S(2)}) async-start(), calls=%async_computation.1 | async-start | bytes 10895360 | tf_op jit(solution)/shard_map/all_gather | solution.py:32
  9.4 631.2 %reduce-scatter.2.cloned.1.call-start = ((), (), s32[]{:S(2)}) async-start(), calls=%async_computation.4 | async-start | bytes 32686080 | tf_op jit(solution)/shard_map/reduce_scatter | solution.py:33
  490.8 102.9 %slice-start = ((s8[8716288]{0:T(1024)(128)(4,1)}), s8[327680]{0:T(1024)(128)(4,1)S(1)}, s32[]{:S(2)}) async-start(s8[8716288]{0:T(1024)(128)(4,1)} %bitcast.38), calls=%async_computation.5 | async-start | bytes 655360
  543.7 50.0 %slice-start.1 = ((s8[8716288]{0:T(1024)(128)(4,1)}), s8[4194304]{0:T(1024)(128)(4,1)S(1)}, s32[]{:S(2)}) async-start(s8[8716288]{0:T(1024)(128)(4,1)} %bitcast.38), calls=%async_computation.6 | async-start | bytes 8388608
  543.7 50.0 %slice-start.2 = ((s8[8716288]{0:T(1024)(128)(4,1)}), s8[4194304]{0:T(1024)(128)(4,1)S(1)}, s32[]{:S(2)}) async-start(s8[8716288]{0:T(1024)(128)(4,1)} %bitcast.38), calls=%async_computation.7 | async-start | bytes 8388608
Sparse Core Ops, SparseCore 0:
  9.5 60.4 all-gather.7
  71.5 57.6 all-gather.5
  130.7 57.6 all-gather.3
  190.7 174.9 reduce-scatter.1
where the time goes:
time: 954 us; the launch traced here: 948 us
  matrix products  465 us (49%)
  blocking collectives  300 us (31%)
  local copies, waits for them, and re-layouts  94 us (10%)
  waiting for transfers between devices  39.2 us (4%)
  other arithmetic  34.6 us (4%)
  between operations  14 us (1%)
    psum x1, blocking collectives, local_step(): grad_next = lax.psum(g_shard.astype(jnp.float32), 'dp')  300 us
    dot_general x1, matrix products, mlp_backward(): jnp.einsum('td,fd->tf', dy_flat, w_down, preferred_element_type=jnp.float32)  96.9 us
    unnamed x8, local copies, waits for them, and re-layouts  94 us
    dot_general x1, matrix products, mlp_backward(): jnp.einsum('td,tf->df', dy_flat, hidden, preferred_element_type=jnp.float32)  64.9 us
    dot_general x1, matrix products, mlp_backward(): jnp.einsum('td,tf->df', x_flat, d_gate, preferred_element_type=jnp.float32)  53.4 us
    dot_general x1, matrix products, mlp_backward(): jnp.einsum('td,tf->df', x_flat, d_up, preferred_element_type=jnp.float32)  52.8 us
    dot_general x1, matrix products, mlp_backward(): pre_gate = jnp.dot(x_flat, w_gate, preferred_element_type=jnp.float32)  50.3 us
    dot_general x1, matrix products, mlp_backward(): pre_up = jnp.dot(x_flat, w_up, preferred_element_type=jnp.float32)  50.3 us
  transfers between devices with their start and end apart: 4, of which 3 were waited for; matrix products, arithmetic and copies ran while one was open for 63% of the time, Pallas kernels for 0%

commit v1 on v0

v1 whole, which is shorter than its diff:
```python
import jax
import jax.numpy as jnp
from jax import lax
from jax.experimental import pallas as pl
from jax.experimental.pallas import tpu as pltpu
from jax.sharding import PartitionSpec as P

TOK_AXES = ("dp", "row", "fsdp")
GROUP_AXES = ("row", "fsdp")

D = 896
FF = 4864
N = 4096
SH = FF // 4
FT = 256
T = 1024
NF = FF // FT
C = N // T
XB = 512
UN = 42
UR, UC = 128, 640
A0, B0, C0, D0 = 9, 12, 18, 24
PS, QS = C0 - B0 + 1, D0 - C0 + 1
NT = (((1,), (1,)), ((), ()))
F32, BF16 = jnp.float32, jnp.bfloat16
MESH = pl.DeviceIdType.MESH


def step_kernel(x_h, dy_h, w1_h, w3_h, w2_h, g_h,
                dw_h, dx_h, dn_h, wg1, wg3, wg2, ra_h, rx_h, ry_h,
                xt, dyt, acc, wb, wn, dwb, gba, gbb, ob,
                ga, gb_in, sa, ra, pb, rx, qb, ry, tb,
                wsem, dsem, xsem, osem, lsem, agl, ags, agr,
                gas, gbs, ras, rxs, rys, tbs, sas, sar, sxs, sxr, sys_, syr):
    d = lax.axis_index("dp")
    r = lax.axis_index("row")
    c = lax.axis_index("fsdp")
    core = (d, r, 1 - c)
    xnb = (d, 1 - r, c)
    ynb = (1 - d, r, c)
    s = 2 * r + c
    so = 2 * (1 - r) + c

    bar = pltpu.get_barrier_semaphore()
    for dev in (core, xnb, ynb):
        pl.semaphore_signal(bar, inc=1, device_id=dev, device_id_type=MESH)
    pl.semaphore_wait(bar, 3)

    own = (w1_h, w3_h, w2_h)
    full = (wg1, wg3, wg2)

    def rows(start, size):
        return pl.ds(pl.multiple_of(start, 32), size)

    def remote(src, dst, ssem, rsem, dev):
        return pltpu.make_async_remote_copy(src_ref=src, dst_ref=dst, send_sem=ssem, recv_sem=rsem, device_id=dev, device_id_type=MESH)

    H = SH // 2

    def ag(kind, w):
        if kind == 0:
            return remote(own[w], full[w].at[rows(s * SH, SH)], ags.at[kind, w], agr.at[kind, w], core)
        if kind == 1:
            return remote(own[w].at[rows(d * H, H)], full[w].at[rows(s * SH + d * H, H)], ags.at[kind, w], agr.at[kind, w], xnb)
        got = full[w].at[rows(so * SH + d * H, H)]
        if kind == 2:
            return remote(got, got, ags.at[kind, w], agr.at[kind, w], ynb)
        if kind == 3:
            return remote(got, got, ags.at[kind, w], agr.at[kind, w], core)
        got = full[w].at[rows(so * SH + (1 - d) * H, H)]
        return remote(got, got, ags.at[kind, w], agr.at[kind, w], core)

    for w in range(3):
        ag(1, w).start()
    for w in range(3):
        ag(0, w).start()

    def edge(w, e):
        off = e * (SH - 192)
        return pltpu.make_async_copy(own[w].at[rows(off, 192)], full[w].at[rows(s * SH + off, 192)], agl.at[w, e])

    for w in range(3):
        for e in range(2):
            edge(w, e).start()

    def tile(j):
        one = jnp.where(j < 4, 5 + j, jnp.where(j < 9, 8 - j, jnp.where(j < 13, 6 + j, 27 - j)))
        zero = j
        t = jnp.where(r == c, zero, one)
        return jnp.where(r == 1, NF - 1 - t, t)

    def wcopy(j, slot, mine):
        t = tile(j)
        out = []
        for w in range(3):
            if mine:
                src = own[w].at[rows(t * FT - s * SH, FT)]
            else:
                src = full[w].at[rows(t * FT, FT)]
            out.append(pltpu.make_async_copy(src, wb.at[slot, pl.ds(w * FT, FT)], wsem.at[slot, w]))
        return out

    for cp in wcopy(0, 0, True):
        cp.start()
    for cp in wcopy(1, 1, True):
        cp.start()

    nx = N // XB

    def xload(k, src):
        return pltpu.make_async_copy(src.at[pl.ds(pl.multiple_of(k * XB, XB), XB)], ob.at[lax.rem(k, 2)], xsem.at[lax.rem(k, 2)])

    for src, dst in ((x_h, xt), (dy_h, dyt)):
        xload(0, src).start()

        def tr(k, _, src=src, dst=dst):
            @pl.when(k + 1 < nx)
            def _():
                xload(k + 1, src).start()
            xload(k, src).wait()
            dst[:, pl.ds(pl.multiple_of(k * XB, XB), XB)] = ob[lax.rem(k, 2)].T
            return 0
        lax.fori_loop(0, nx, tr, 0)

    def zero(k, _):
        acc[:, pl.ds(pl.multiple_of(k * 256, 256), 256)] = jnp.zeros((D, 256), F32)
        return 0
    lax.fori_loop(0, N // 256, zero, 0)

    def trans(src, dst):
        for k in range(D // 128):
            ck = pl.ds(k * 128, 128)
            wn[dst, ck, 0:FT] = wb[src, 0:FT, ck].T
            wn[dst, ck, FT:2 * FT] = wb[src, FT:2 * FT, ck].T

    def stage1(it, gb):
        j = it // C
        ws = lax.rem(j, 3)
        cols = pl.ds(pl.multiple_of(lax.rem(it, C) * T, T), T)
        ab = jnp.dot(wb[ws, 0:2 * FT, :], xt[:, cols], preferred_element_type=F32)
        dh = jnp.dot(wb[ws, 2 * FT:3 * FT, :], dyt[:, cols], preferred_element_type=F32)
        a = ab[:FT]
        b = ab[FT:]
        sg = jax.nn.sigmoid(a)
        act = a * sg
        gb[2 * FT:3 * FT, :] = (act * b).astype(BF16)
        gb[FT:2 * FT, :] = (dh * act).astype(BF16)
        gb[0:FT, :] = (dh * b * sg * (1.0 + a * (1.0 - sg))).astype(BF16)

    def stage2(it, gb):
        ck = lax.rem(it, C)
        ns = lax.rem(it // C, 2)
        cols = pl.ds(pl.multiple_of(ck * T, T), T)
        acc[:, cols] += jnp.dot(wn[ns], gb[0:2 * FT, :], preferred_element_type=F32)
        d1 = lax.dot_general(xt[:, cols], gb[0:2 * FT, :], NT, preferred_element_type=F32)
        d2 = lax.dot_general(dyt[:, cols], gb[2 * FT:3 * FT, :], NT, preferred_element_type=F32)
        first = ck == 0
        dwb[ns, 0] = jnp.where(first, 0.0, dwb[ns, 0]) + d1[:, :FT]
        dwb[ns, 1] = jnp.where(first, 0.0, dwb[ns, 1]) + d1[:, FT:]
        dwb[ns, 2] = jnp.where(first, 0.0, dwb[ns, 2]) + d2

    def dcopy(j):
        sl = lax.rem(j, 2)
        return pltpu.make_async_copy(dwb.at[sl], dw_h.at[:, :, pl.ds(pl.multiple_of(tile(j) * FT, 128), FT)], dsem.at[sl])

    def ocopy(k):
        return pltpu.make_async_copy(ob.at[lax.rem(k, 2)], dx_h.at[pl.ds(pl.multiple_of(k * XB, XB), XB)], osem.at[lax.rem(k, 2)])

    def unit(u):
        return u // 14, lax.rem(u, 14) // 2, lax.rem(u, 2)

    def gload(u, cc, buf, sem):
        k, i, h = unit(u)
        sl = lax.rem(u, 2)
        out = []
        for q in range(2):
            col = q * (FF // 2) + cc * 1152 + h * UC
            out.append(pltpu.make_async_copy(g_h.at[k, pl.ds(pl.multiple_of(i * UR, UR), UR), pl.ds(pl.multiple_of(col, 128), UC)], buf.at[sl, q], sem.at[sl, q]))
        return out

    def load_a(u):
        return gload(u, 1 - c, ga, gas)

    def load_b(u):
        return gload(u, c, gb_in, gbs) + [pltpu.make_async_copy(ra_h.at[u], ra.at[lax.rem(u, 2)], ras.at[lax.rem(u, 2)])]

    def send_a(u):
        return remote(sa.at[lax.rem(u, 3)], ra_h.at[u], sas.at[u], sar.at[u], core)

    def send_x(u):
        return remote(pb.at[lax.rem(u, PS), 1 - r], rx_h.at[u], sxs.at[u], sxr.at[u], xnb)

    def send_y(u):
        return remote(qb.at[lax.rem(u, QS)], ry_h.at[u], sys_.at[u], syr.at[u], ynb)

    def load_c(u):
        return pltpu.make_async_copy(rx_h.at[u], rx.at[lax.rem(u, 2)], rxs.at[lax.rem(u, 2)])

    def load_d(u):
        return pltpu.make_async_copy(ry_h.at[u], ry.at[lax.rem(u, 2)], rys.at[lax.rem(u, 2)])

    def out_d(bk):
        sl = lax.rem(bk, 2)
        return pltpu.make_async_copy(tb.at[sl, pl.ds(pl.multiple_of(64 * c, 64), SH)], dn_h.at[bk // 7, :, pl.ds(pl.multiple_of(lax.rem(bk, 7) * UR, UR), UR)], tbs.at[sl])

    def on(u):
        return (u >= 0) & (u < UN)

    def background(it):
        for w in range(3):
            @pl.when(it == 8 + 5 * w)
            def _(w=w):
                ag(1, w).wait_recv()
                ag(2, w).start()
                ag(3, w).start()

            @pl.when(it == 15 + 5 * w)
            def _(w=w):
                ag(2, w).wait_recv()
                ag(4, w).start()
        ua, ub, uc, ud = it - A0, it - B0, it - C0, it - D0

        @pl.when(on(ua - 1))
        def _():
            send_a(ua - 1).start()

        @pl.when(on(ub - 1))
        def _():
            send_x(ub - 1).start()

        @pl.when(on(uc - 1))
        def _():
            send_y(uc - 1).start()

        @pl.when(on(ua + 1))
        def _():
            for cp in load_a(ua + 1):
                cp.start()

        @pl.when(on(ub + 1))
        def _():
            send_a(ub + 1).wait_recv()
            for cp in load_b(ub + 1):
                cp.start()

        @pl.when(on(uc + 1))
        def _():
            send_x(uc + 1).wait_recv()
            load_c(uc + 1).start()

        @pl.when(on(ud + 1))
        def _():
            send_y(ud + 1).wait_recv()
            load_d(ud + 1).start()

        @pl.when(on(ua))
        def _():
            @pl.when(ua >= 3)
            def _():
                send_a(ua - 3).wait_send()
            for cp in load_a(ua):
                cp.wait()
            sa[lax.rem(ua, 3)] = ga[lax.rem(ua, 2)].astype(BF16)

        @pl.when(on(ub))
        def _():
            @pl.when(ub >= PS)
            def _():
                send_x(ub - PS).wait_send()
            for cp in load_b(ub):
                cp.wait()
            sl = lax.rem(ub, 2)
            pb[lax.rem(ub, PS)] = (gb_in[sl].astype(BF16).astype(F32) + ra[sl].astype(F32)).astype(BF16)

        @pl.when(on(uc))
        def _():
            @pl.when(uc >= QS)
            def _():
                send_y(uc - QS).wait_send()
            load_c(uc).wait()
            qb[lax.rem(uc, QS)] = (pb[lax.rem(uc, PS), r].astype(F32) + rx[lax.rem(uc, 2)].astype(F32)).astype(BF16)

        @pl.when(on(ud))
        def _():
            bk = ud // 2
            h = lax.rem(ud, 2)

            @pl.when((h == 0) & (bk >= 2))
            def _():
                out_d(bk - 2).wait()
            load_d(ud).wait()
            tot = qb[lax.rem(ud, QS)].astype(F32) + ry[lax.rem(ud, 2)].astype(F32)
            tb[lax.rem(bk, 2), pl.ds(pl.multiple_of(h * UC, 128), UC), :] = tot.T

            @pl.when(h == 1)
            def _():
                out_d(bk).start()

    for cp in wcopy(0, 0, True):
        cp.wait()
    trans(0, 0)
    stage1(0, gba)

    def body(it, src, dst):
        j = it // C
        ck = lax.rem(it, C)
        jp = (it - 1) // C
        cp_ = lax.rem(it - 1, C)

        @pl.when((ck == 1) & (j + 1 < NF) & (j > 0))
        def _():
            @pl.when(j + 1 < 4)
            def _():
                for cp in wcopy(j + 1, lax.rem(j + 1, 3), True):
                    cp.start()

            @pl.when(j + 1 >= 4)
            def _():
                @pl.when(j + 1 == 4)
                def _():
                    for w in range(3):
                        for e in range(2):
                            edge(w, e).wait()
                        ag(0, w).wait_recv()

                @pl.when(j + 1 == 9)
                def _():
                    for w in range(3):
                        ag(3, w).wait_recv()
                        ag(4, w).wait_recv()
                for cp in wcopy(j + 1, lax.rem(j + 1, 3), False):
                    cp.start()

        background(it)

        @pl.when((ck == 0) & (j < NF))
        def _():
            for cp in wcopy(j, lax.rem(j, 3), False):
                cp.wait()
            trans(lax.rem(j, 3), lax.rem(j, 2))

        @pl.when((cp_ == 0) & (jp >= 2))
        def _():
            dcopy(jp - 2).wait()
        stage1(it, dst)
        stage2(it - 1, src)

        @pl.when(cp_ == C - 1)
        def _():
            dcopy(jp).start()

        @pl.when(jp == NF - 1)
        def _():
            for q in range(T // XB):
                k = cp_ * (T // XB) + q

                @pl.when(k >= 2)
                def _():
                    ocopy(k - 2).wait()
                ob[q % 2] = acc[:, pl.ds(pl.multiple_of(k * XB, XB), XB)].astype(BF16).T
                ocopy(k).start()

    def pair(i, _):
        body(2 * i + 1, gba, gbb)
        body(2 * i + 2, gbb, gba)
        return 0
    lax.fori_loop(0, NF * C // 2, pair, 0)

    dcopy(NF - 2).wait()
    dcopy(NF - 1).wait()
    ocopy(N // XB - 2).wait()
    ocopy(N // XB - 1).wait()
    out_d(19).wait()
    out_d(20).wait()
    for w in range(3):
        for kind in range(5):
            ag(kind, w).wait_send()
    for u in range(UN - 3, UN):
        send_a(u).wait_send()
    for u in range(UN - PS, UN):
        send_x(u).wait_send()
    for u in range(UN - QS, UN):
        send_y(u).wait_send()


def solution(mesh):
    def local_step(x_dev, dy_dev, gate_shard, up_shard, down_shard, g_dev):
        any_spec = pl.BlockSpec(memory_space=pl.ANY)
        sds = jax.ShapeDtypeStruct
        dma = pltpu.SemaphoreType.DMA
        vm = pltpu.VMEM
        outs = pl.pallas_call(
            step_kernel,
            in_specs=[any_spec] * 6,
            out_specs=[any_spec] * 9,
            out_shape=[sds((3, D, FF), F32), sds((N, D), BF16), sds((3, SH, D), F32),
                       sds((FF, D), BF16), sds((FF, D), BF16), sds((FF, D), BF16),
                       sds((UN, 2, UR, UC), BF16), sds((UN, UR, UC), BF16), sds((UN, UR, UC), BF16)],
            scratch_shapes=[
                vm((D, N), BF16), vm((D, N), BF16), vm((D, N), F32),
                vm((3, 3 * FT, D), BF16), vm((2, D, 2 * FT), BF16), vm((2, 3, D, FT), F32),
                vm((3 * FT, T), BF16), vm((3 * FT, T), BF16), vm((2, XB, D), BF16),
                vm((2, 2, UR, UC), F32), vm((2, 2, UR, UC), F32), vm((3, 2, UR, UC), BF16),
                vm((2, 2, UR, UC), BF16), vm((PS, 2, UR, UC), BF16), vm((2, UR, UC), BF16),
                vm((QS, UR, UC), BF16), vm((2, UR, UC), BF16), vm((2, 2 * UC, UR), F32),
                dma((3, 3)), dma((2,)), dma((2,)), dma((2,)), dma((1,)), dma((3, 2)), dma((5, 3)), dma((5, 3)),
                dma((2, 2)), dma((2, 2)), dma((2,)), dma((2,)), dma((2,)), dma((2,)),
                dma((UN,)), dma((UN,)), dma((UN,)), dma((UN,)), dma((UN,)), dma((UN,)),
            ],
            compiler_params=pltpu.CompilerParams(collective_id=0, has_side_effects=True, vmem_limit_bytes=65470 * 1024),
        )(x_dev.reshape(N, D), dy_dev.reshape(N, D), gate_shard.T, up_shard.T, down_shard, g_dev[0])
        dw, dx, dn = outs[:3]
        return dx.reshape(2, N // 2, D), dn.transpose(0, 2, 1), dw[None]

    in_specs = (P(None, TOK_AXES, None), P(None, TOK_AXES, None), P(None, GROUP_AXES), P(None, GROUP_AXES), P(GROUP_AXES, None), P(TOK_AXES, None, None, None))
    out_specs = (P(None, TOK_AXES, None), P(None, None, GROUP_AXES), P(TOK_AXES, None, None, None))
    return jax.shard_map(local_step, mesh=mesh, in_specs=in_specs, out_specs=out_specs, check_vma=False)
```

time: 954 us -> 455 us (0.48)
  matrix products: 465 us -> 0 us
  Pallas kernels: 0 us -> 403 us
  blocking collectives: 300 us -> 0 us
  local copies, waits for them, and re-layouts: 94 us -> 50.9 us
  waiting for transfers between devices: 39.2 us -> 0 us
  other arithmetic: 34.6 us -> 0 us
  between operations: 14 us -> 0.64 us
    dot_general x8 -> x0, matrix products: 465 us -> none  [the longest x1 96.9 us: mlp_backward(): jnp.einsum('td,fd->tf', dy_flat, w_down, preferred_element_type=jnp.float32)]
    pallas_call x0 -> x1, Pallas kernels: none -> 403 us  [local_step(): pl.pallas_call(step_kernel, in_specs=[any_spec] * 6, out_specs=[any_spec]...]
    psum x1 -> x0, blocking collectives: 300 us -> none  [local_step(): grad_next = lax.psum(g_shard.astype(jnp.float32), 'dp')]
    unnamed x8 -> x3, local copies, waits for them, and re-layouts: 94 us -> 50.9 us
    all_gather x3 -> x0, waiting for transfers between devices: 37.1 us -> none  [the longest x1 19.4 us: local_step(): w_gate = lax.all_gather(gate_shard, GROUP_AXES, axis=1, tiled=True)]
    broadcast_in_dim x1 -> x0, other arithmetic: 34.6 us -> none  [local_step(): grad_layer[None]]
  transfers between devices with their start and end apart: 4 -> 0, of which waited for: 3 -> 0; matrix products, arithmetic and copies ran while one was open for 63% -> 0% of each run, Pallas kernels for 0% -> 0%
where the time goes in v1:
time: 455 us
  Pallas kernels  403 us (89%)
  local copies, waits for them, and re-layouts  50.9 us (11%)
    pallas_call x1, Pallas kernels, local_step(): pl.pallas_call(step_kernel, in_specs=[any_spec] * 6, out_specs=[any_spec]...  403 us
    unnamed x3, local copies, waits for them, and re-layouts  50.9 us

profile of v1, /device:TPU:0, one launch (start us, length us, event | category | flops | bytes accessed | tf_op | source)
XLA Modules:
  0.0 454.8 jit_solution(2529163126429225152)
XLA Ops:
  0.6 403.3 %shard_map.85 = (f32[3,896,4864]{2,1,0:T(8,128)}, bf16[4096,896]{1,0:T(8,128)(2,1)}, f32[3,1216,896]{2,1,0:T(8,128)}, bf16[4864,896]{1,0:T(8,128)(2,1)}, bf16[48...) custom-call(bf16[4096,896]{1,0:T(8,128)(2,1)} %bitcast.12, ...), custom_call_target="tpu_custom_call" | custom-call | tf_op jit(solution)/shard_map/pallas_call | solution.py:392
  403.9 6.7 %copy.12 = bf16[2,2048,896]{2,1,0:T(8,128)(2,1)} copy(bf16[2,2048,896]{2,1,0:T(8,128)(2,1)} %bitcast.11) | data formatting | bytes 14680064
  410.6 10.5 %copy.13 = f32[3,896,1216]{1,2,0:T(8,128)} copy(f32[3,896,1216]{1,2,0:T(8,128)} %bitcast.10) | data formatting | bytes 26148864
  421.1 33.6 %copy.14 = f32[1,3,896,4864]{3,2,1,0:T(8,128)} copy(f32[1,3,896,4864]{3,2,1,0:T(8,128)} %bitcast.8) | data formatting | bytes 104595456

commit v2 on v1

v2 whole, which is shorter than its diff:
```python
import functools

import jax
import jax.numpy as jnp
from jax import lax
from jax.experimental import pallas as pl
from jax.experimental.pallas import tpu as pltpu
from jax.sharding import PartitionSpec as P

TOK_AXES = ("dp", "row", "fsdp")
GROUP_AXES = ("row", "fsdp")

D = 896
FF = 4864
N = 4096
SH = FF // 4
FT = 256
T = 1024
NF = FF // FT
TW = 512
NW = FF // TW
TL = FF - NW * TW
C = N // T
TP = 512
XS = 6
XB = 256
UN = 21
UR, UC = 128, 1280
A0, B0, C0, D0 = 6, 8, 11, 14
PS, QS = C0 - B0 + 1, D0 - C0 + 1
NT = (((1,), (1,)), ((), ()))
F32, BF16 = jnp.float32, jnp.bfloat16
MESH = pl.DeviceIdType.MESH


def step_kernel(x_h, dy_h, w1_h, w3_h, w2_h, g_h,
                dw_h, dx_h, dn_h, wg1, wg3, wg2, ra_h, rx_h, ry_h, db_h, hh_h, xt_h, dyt_h,
                xt, dyt, acc, wb, wn, dwb, gba, gbb, raw2, ob,
                ga, gb_in, sa, ra, pb, rx, qb, ry, tb,
                wsem, dsem, xsem, osem, lsem, agl, ags, agr,
                gas, gbs, ras, rxs, rys, tbs, gos, xos, sas, sar, sxs, sxr, sys_, syr):
    d = lax.axis_index("dp")
    r = lax.axis_index("row")
    c = lax.axis_index("fsdp")
    core = (d, r, 1 - c)
    xnb = (d, 1 - r, c)
    ynb = (1 - d, r, c)
    s = 2 * r + c
    so = 2 * (1 - r) + c

    bar = pltpu.get_barrier_semaphore()
    for dev in (core, xnb, ynb):
        pl.semaphore_signal(bar, inc=1, device_id=dev, device_id_type=MESH)
    pl.semaphore_wait(bar, 3)

    own = (w1_h, w3_h, w2_h)
    full = (wg1, wg3, wg2)

    def rows(start, size):
        return pl.ds(pl.multiple_of(start, 32), size)

    def remote(src, dst, ssem, rsem, dev):
        return pltpu.make_async_remote_copy(src_ref=src, dst_ref=dst, send_sem=ssem, recv_sem=rsem, device_id=dev, device_id_type=MESH)

    H = SH // 2

    def ag(kind, w):
        if kind == 0:
            return remote(own[w], full[w].at[rows(s * SH, SH)], ags.at[kind, w], agr.at[kind, w], core)
        if kind == 1:
            return remote(own[w].at[rows(d * H, H)], full[w].at[rows(s * SH + d * H, H)], ags.at[kind, w], agr.at[kind, w], xnb)
        got = full[w].at[rows(so * SH + d * H, H)]
        if kind == 2:
            return remote(got, got, ags.at[kind, w], agr.at[kind, w], ynb)
        if kind == 3:
            return remote(got, got, ags.at[kind, w], agr.at[kind, w], core)
        got = full[w].at[rows(so * SH + (1 - d) * H, H)]
        return remote(got, got, ags.at[kind, w], agr.at[kind, w], core)

    for w in range(3):
        ag(1, w).start()
    for w in range(3):
        ag(0, w).start()

    def edge(w, e):
        off = e * (SH - 192)
        return pltpu.make_async_copy(own[w].at[rows(off, 192)], full[w].at[rows(s * SH + off, 192)], agl.at[w, e])

    for w in range(3):
        for e in range(2):
            edge(w, e).start()

    def tile(j):
        one = jnp.where(j < 4, 5 + j, jnp.where(j < 9, 8 - j, jnp.where(j < 13, 6 + j, 27 - j)))
        zero = j
        t = jnp.where(r == c, zero, one)
        return jnp.where(r == 1, NF - 1 - t, t)

    def wcopy(j, slot, mine):
        t = tile(j)
        out = []
        for w in range(3):
            if mine:
                src = own[w].at[rows(t * FT - s * SH, FT)]
            else:
                src = full[w].at[rows(t * FT, FT)]
            out.append(pltpu.make_async_copy(src, wb.at[slot, pl.ds(w * FT, FT)], wsem.at[slot, w]))
        return out

    for cp in wcopy(0, 0, True):
        cp.start()
    for cp in wcopy(1, 1, True):
        cp.start()

    nx = N // XB

    def xload(k, act):
        sl = lax.rem(k, XS)
        rs = pl.ds(pl.multiple_of(lax.rem(k, nx) * XB, XB), XB)

        @pl.when(k < nx)
        def _():
            getattr(pltpu.make_async_copy(x_h.at[rs], ob.at[sl], xsem.at[sl]), act)()

        @pl.when(k >= nx)
        def _():
            getattr(pltpu.make_async_copy(dy_h.at[rs], ob.at[sl], xsem.at[sl]), act)()

    for k in range(XS - 1):
        xload(k, "start")

    def tr(k, _, dst=None):
        @pl.when(k + XS - 1 < 2 * nx)
        def _():
            xload(k + XS - 1, "start")
        xload(k, "wait")
        dst[:, pl.ds(pl.multiple_of(lax.rem(k, nx) * XB, XB), XB)] = ob[lax.rem(k, XS)].T
        return 0
    lax.fori_loop(0, nx, functools.partial(tr, dst=xt), 0)
    lax.fori_loop(nx, 2 * nx, functools.partial(tr, dst=dyt), 0)

    keep = (pltpu.make_async_copy(xt, xt_h, xos.at[0]), pltpu.make_async_copy(dyt, dyt_h, xos.at[1]))
    for cp in keep:
        cp.start()

    def zero(k, _):
        acc[:, pl.ds(pl.multiple_of(k * 256, 256), 256)] = jnp.zeros((D, 256), F32)
        return 0
    lax.fori_loop(0, N // 256, zero, 0)

    def trans(src, dst, k):
        ck = pl.ds(pl.multiple_of(k * 128, 128), 128)
        wn[dst, ck, 0:FT] = wb[src, 0:FT, ck].T
        wn[dst, ck, FT:2 * FT] = wb[src, FT:2 * FT, ck].T

    def products(it, raw):
        ck = lax.rem(it, C)
        ws = lax.rem(it // C, 3)

        def piece(half, p):
            to = pl.ds(p * TP, TP)
            cols = pl.ds(pl.multiple_of(ck * T + p * TP, TP), TP)
            if half == 0:
                raw[0:2 * FT, to] = jnp.dot(wb[ws, 0:2 * FT, :], xt[:, cols], preferred_element_type=F32)
            else:
                raw[2 * FT:3 * FT, to] = jnp.dot(wb[ws, 2 * FT:3 * FT, :], dyt[:, cols], preferred_element_type=F32)
        return [functools.partial(piece, half, p) for half in range(2) for p in range(T // TP)]

    def gates(raw, gb):
        def piece(i, p):
            to = pl.ds(p * 512, 512)
            a = raw[pl.ds(i * 16, 16), to]
            b = raw[pl.ds(FT + i * 16, 16), to]
            dh = raw[pl.ds(2 * FT + i * 16, 16), to]
            sg = jax.nn.sigmoid(a)
            act = a * sg
            gb[pl.ds(2 * FT + i * 16, 16), to] = (act * b).astype(BF16)
            gb[pl.ds(FT + i * 16, 16), to] = (dh * act).astype(BF16)
            gb[pl.ds(i * 16, 16), to] = (dh * b * sg * (1.0 + a * (1.0 - sg))).astype(BF16)
        return [functools.partial(piece, i, p) for p in range(T // 512) for i in range(FT // 16)]

    def add_dx(it, gb):
        ck = lax.rem(it, C)
        ns = lax.rem(it // C, 3)

        def piece(p):
            cols = pl.ds(pl.multiple_of(ck * T + p * TP, TP), TP)
            acc[:, cols] += jnp.dot(wn[ns], gb[0:2 * FT, p * TP:(p + 1) * TP], preferred_element_type=F32)
        return [functools.partial(piece, p) for p in range(T // TP)]

    def add_dw(it, gb):
        ck = lax.rem(it, C)
        ns = lax.rem(it // C, 2)
        cols = pl.ds(pl.multiple_of(ck * T, T), T)

        def piece(p):
            mr = pl.ds(p * (D // 2), D // 2)
            d0 = lax.dot_general(xt[mr, cols], gb[0:FT, :], NT, preferred_element_type=F32)
            dwb[ns, mr] = jnp.where(ck == 0, 0.0, dwb[ns, mr]) + d0
        return [functools.partial(piece, p) for p in range(2)]

    def dcopy(j):
        sl = lax.rem(j, 2)
        return pltpu.make_async_copy(dwb.at[sl], dw_h.at[:, pl.ds(pl.multiple_of(tile(j) * FT, 128), FT)], dsem.at[sl])

    def gcopy(it, gb, sl):
        rs = rows(tile(it // C) * FT, FT)
        cs = pl.ds(pl.multiple_of(lax.rem(it, C) * T, T), T)
        return [pltpu.make_async_copy(gb.at[pl.ds(FT, FT)], db_h.at[rs, cs], gos.at[sl, 0]),
                pltpu.make_async_copy(gb.at[pl.ds(2 * FT, FT)], hh_h.at[rs, cs], gos.at[sl, 1])]

    def ocopy(k):
        return pltpu.make_async_copy(ob.at[lax.rem(k, 2)], dx_h.at[pl.ds(pl.multiple_of(k * XB, XB), XB)], osem.at[lax.rem(k, 2)])

    def unit(u):
        return u // 7, lax.rem(u, 7)

    def gload(u, cc, buf, sem):
        k, i = unit(u)
        out = []
        for q in range(2):
            col = q * (FF // 2) + cc * 1152
            out.append(pltpu.make_async_copy(g_h.at[k, pl.ds(pl.multiple_of(i * UR, UR), UR), pl.ds(pl.multiple_of(col, 128), UC)], buf.at[q], sem.at[q]))
        return out

    def load_a(u):
        return gload(u, 1 - c, ga, gas)

    def load_b(u):
        return gload(u, c, gb_in, gbs) + [pltpu.make_async_copy(ra_h.at[u], ra, ras.at[0])]

    def send_a(u):
        return remote(sa.at[lax.rem(u, 2)], ra_h.at[u], sas.at[u], sar.at[u], core)

    def send_x(u):
        return remote(pb.at[lax.rem(u, PS), 1 - r], rx_h.at[u], sxs.at[u], sxr.at[u], xnb)

    def send_y(u):
        return remote(qb.at[lax.rem(u, QS)], ry_h.at[u], sys_.at[u], syr.at[u], ynb)

    def load_c(u):
        return pltpu.make_async_copy(rx_h.at[u], rx, rxs.at[0])

    def load_d(u):
        return pltpu.make_async_copy(ry_h.at[u], ry, rys.at[0])

    def out_d(u):
        sl = lax.rem(u, 2)
        return pltpu.make_async_copy(tb.at[sl, pl.ds(pl.multiple_of(64 * c, 64), SH)], dn_h.at[u // 7, :, pl.ds(pl.multiple_of(lax.rem(u, 7) * UR, UR), UR)], tbs.at[sl])

    def on(u):
        return (u >= 0) & (u < UN)

    def forward(it):
        for w in range(3):
            @pl.when(it == 6 + 6 * w)
            def _(w=w):
                ag(1, w).wait_recv()
                ag(2, w).start()
                ag(3, w).start()

            @pl.when(it == (14, 20, 28)[w])
            def _(w=w):
                ag(2, w).wait_recv()
                ag(4, w).start()

    def first_half(i):
        ua, ub, uc, ud = i - A0, i - B0, i - C0, i - D0

        @pl.when(on(uc - 1))
        def _():
            send_y(uc - 1).start()

        @pl.when(on(uc))
        def _():
            send_x(uc).wait_recv()
            load_c(uc).start()

        @pl.when(on(ud))
        def _():
            send_y(ud).wait_recv()
            load_d(ud).start()

        @pl.when(on(ua))
        def _():
            @pl.when(ua >= 2)
            def _():
                send_a(ua - 2).wait_send()
            for cp in load_a(ua):
                cp.wait()

        @pl.when(on(ub))
        def _():
            @pl.when(ub >= PS)
            def _():
                send_x(ub - PS).wait_send()
            for cp in load_b(ub):
                cp.wait()

    def second_half(i):
        ua, ub, uc, ud = i - A0, i - B0, i - C0, i - D0

        @pl.when(on(ua))
        def _():
            send_a(ua).start()

        @pl.when(on(ub))
        def _():
            send_x(ub).start()

        @pl.when(on(ua + 1))
        def _():
            for cp in load_a(ua + 1):
                cp.start()

        @pl.when(on(ub + 1))
        def _():
            send_a(ub + 1).wait_recv()
            for cp in load_b(ub + 1):
                cp.start()

        @pl.when(on(uc))
        def _():
            @pl.when(uc >= QS)
            def _():
                send_y(uc - QS).wait_send()
            load_c(uc).wait()

        @pl.when(on(ud))
        def _():
            @pl.when(ud >= 2)
            def _():
                out_d(ud - 2).wait()
            load_d(ud).wait()

    def mod(u, n):
        return lax.rem(u + 40 * n, n)

    def spot(u, n):
        return jnp.where(on(u), mod(u, n), n)

    def arith_ab(i):
        da, db = spot(i - A0, 2), spot(i - B0, PS)

        def cast(q, n):
            rs = pl.ds(n * 16, 16)
            sa[da, q, rs] = ga[q, rs].astype(BF16)

        def core_sum(q, n):
            rs = pl.ds(n * 16, 16)
            pb[db, q, rs] = (gb_in[q, rs].astype(BF16).astype(F32) + ra[q, rs].astype(F32)).astype(BF16)
        return [functools.partial(f, q, n) for q in range(2) for n in range(UR // 16) for f in (cast, core_sum)]

    def arith_cd(i):
        uc, ud = i - C0, i - D0
        dc, dd = spot(uc, QS), spot(ud, 2)

        def row_sum(n):
            rs = pl.ds(n * 16, 16)
            qb[dc, rs] = (pb[mod(uc, PS), r, rs].astype(F32) + rx[rs].astype(F32)).astype(BF16)

        def dp_sum(n):
            cs = pl.ds(n * 128, 128)
            tot = qb[mod(ud, QS), :, cs].astype(F32) + ry[:, cs].astype(F32)
            tb[dd, pl.ds(n * 128, 128), :] = tot.T
        return [functools.partial(dp_sum, n) for n in range(UC // 128)] + [functools.partial(row_sum, n) for n in range(UR // 16)]

    def flush(i):
        @pl.when(on(i - D0))
        def _():
            out_d(i - D0).start()

    for cp in wcopy(0, 0, True):
        cp.wait()
    for k in range(D // 128):
        trans(0, 0, k)
    for cp in wcopy(1, 1, True):
        cp.wait()
    for k in range(2):
        trans(1, 1, k)
    gbs2 = (gba, gbb)

    def body(it, par, step=None):
        j = it // C
        ck = lax.rem(it, C)
        jp = (it - 1) // C
        cp_ = lax.rem(it - 1, C)
        jn = j + 2

        @pl.when((ck == 1) & (jn < NF))
        def _():
            @pl.when(jn < 4)
            def _():
                for cp in wcopy(jn, lax.rem(jn, 3), True):
                    cp.start()

            @pl.when(jn >= 4)
            def _():
                @pl.when(jn == 4)
                def _():
                    for w in range(3):
                        for e in range(2):
                            edge(w, e).wait()
                        ag(0, w).wait_recv()

                @pl.when(jn == 9)
                def _():
                    for w in range(3):
                        ag(3, w).wait_recv()
                        ag(4, w).wait_recv()
                for cp in wcopy(jn, lax.rem(jn, 3), False):
                    cp.start()

        @pl.when((ck == 0) & (j + 1 < NF))
        def _():
            for cp in wcopy(j + 1, lax.rem(j + 1, 3), False):
                cp.wait()

        side = []
        if step is not None:
            if par == 0:
                forward(it)
                first_half(step)
                side = arith_ab(step)
            else:
                second_half(step)
                side = arith_cd(step)
        for cp in gcopy(it - 1, gbs2[1 - par], 1 - par):
            cp.start()

        @pl.when(it >= 2)
        def _():
            for cp in gcopy(it - 2, gbs2[par], par):
                cp.wait()

        @pl.when((cp_ == 0) & (jp >= 2))
        def _():
            dcopy(jp - 2).wait()
        prod, gate = products(it, raw2), gates(raw2, gbs2[par])
        grad = add_dx(it - 1, gbs2[1 - par]) + add_dw(it - 1, gbs2[1 - par])
        side += [functools.partial(trans, lax.rem(j + 1, 3), lax.rem(j + 1, 3), jnp.minimum(2 * ck + q, D // 128 - 1)) for q in range(2)]
        ng, nd = len(gate) // 2, len(side) // 2
        run(prod[0], prod[2], prod[1], *gate[:ng], prod[3], *side[:nd], *grad[:1], *gate[ng:], *grad[1:2], *side[nd:], *grad[2:])
        if step is not None and par == 1:
            flush(step)
        grads_out(jp, cp_)

    def run(*fs):
        for f in fs:
            f()

    def grads_out(jp, cp_):
        @pl.when(cp_ == C - 1)
        def _():
            dcopy(jp).start()

        @pl.when(jp == NF - 1)
        def _():
            for q in range(T // XB):
                k = cp_ * (T // XB) + q

                @pl.when(k >= 2)
                def _():
                    ocopy(k - 2).wait()
                ob[q % 2] = acc[:, pl.ds(pl.multiple_of(k * XB, XB), XB)].astype(BF16).T
                ocopy(k).start()

    run(*products(0, raw2), *gates(raw2, gba))
    body(1, 1)

    def pair(i, _):
        body(2 * i + 2, 0, i)
        body(2 * i + 3, 1, i)
        return 0
    lax.fori_loop(0, NF * C // 2 - 1, pair, 0)
    last = NF * C - 1
    for cp in gcopy(last, gbb, 1):
        cp.start()
    for cp in gcopy(last - 1, gba, 0):
        cp.wait()
    run(*add_dx(last, gbb), *add_dw(last, gbb))
    grads_out(NF - 1, C - 1)

    dcopy(NF - 2).wait()
    dcopy(NF - 1).wait()
    for cp in gcopy(NF * C - 1, gbb, 1):
        cp.wait()
    for cp in keep:
        cp.wait()
    ocopy(N // XB - 2).wait()
    ocopy(N // XB - 1).wait()
    out_d(19).wait()
    out_d(20).wait()
    for w in range(3):
        for kind in range(5):
            ag(kind, w).wait_send()
    for u in range(UN - 2, UN):
        send_a(u).wait_send()
    for u in range(UN - PS, UN):
        send_x(u).wait_send()
    for u in range(UN - QS, UN):
        send_y(u).wait_send()


def tail_kernel(xt_h, dyt_h, db_h, hh_h, d0_h, dxi_h, dni_h, dw_h, dx_h, dn_h,
                xt, dyt, db, hh, ow, bx, bn, xsem, gsem, osem, dsem, bsem, csem):
    def part(j, width):
        return pl.ds(pl.multiple_of(j * TW, TW), width)

    def loads(j, width):
        sl = lax.rem(j, 2)
        to = pl.ds(0, width)
        return [pltpu.make_async_copy(db_h.at[part(j, width)], db.at[sl, to], gsem.at[sl, 0]),
                pltpu.make_async_copy(hh_h.at[part(j, width)], hh.at[sl, to], gsem.at[sl, 1])]

    def slab0(j, width):
        sl = lax.rem(j, 2)
        return pltpu.make_async_copy(d0_h.at[:, part(j, width)], ow.at[sl, 0, :, pl.ds(0, width)], dsem.at[sl])

    def out(j, width):
        sl = lax.rem(j, 2)
        return pltpu.make_async_copy(ow.at[sl, :, :, pl.ds(0, width)], dw_h.at[:, :, part(j, width)], osem.at[sl])

    def carry(j, put):
        sl = lax.rem(j, 2)
        rx = pl.ds(pl.multiple_of(j * (N // 8), 128), N // 8)
        rn = pl.ds(pl.multiple_of(j * (SH // 8), 8), SH // 8)
        if put:
            return (pltpu.make_async_copy(bx.at[sl], dx_h.at[rx], csem.at[sl, 0]),
                    pltpu.make_async_copy(bn.at[sl], dn_h.at[:, rn], csem.at[sl, 1]))
        return (pltpu.make_async_copy(dxi_h.at[rx], bx.at[sl], bsem.at[sl, 0]),
                pltpu.make_async_copy(dni_h.at[:, rn], bn.at[sl], bsem.at[sl, 1]))

    ldx = pltpu.make_async_copy(xt_h, xt, xsem.at[0])
    ldy = pltpu.make_async_copy(dyt_h, dyt, xsem.at[1])
    first = loads(0, TW)
    first[0].start()
    ldx.start()
    first[1].start()
    ldy.start()
    slab0(0, TW).start()
    for cp in carry(0, False):
        cp.start()

    def step(j, _):
        sl = lax.rem(j, 2)

        @pl.when(j == 0)
        def _():
            ldx.wait()
            ldy.wait()

        @pl.when((j >= 1) & (j <= 8))
        def _():
            for cp in carry(j - 1, False):
                cp.wait()
            for cp in carry(j - 1, True):
                cp.start()

        @pl.when(j < NW - 1)
        def _():
            for cp in loads(j + 1, TW):
                cp.start()

        @pl.when(j == NW - 1)
        def _():
            for cp in loads(j + 1, TL):
                cp.start()
        for cp in loads(j, TW):
            cp.wait()
        ow[sl, 1] = lax.dot_general(xt[...], db[sl], NT, preferred_element_type=F32)

        @pl.when(j >= 1)
        def _():
            out(j - 1, TW).wait()
            for cp in carry(j - 1, True):
                cp.wait()

        @pl.when(j < NW - 1)
        def _():
            slab0(j + 1, TW).start()

        @pl.when(j == NW - 1)
        def _():
            slab0(j + 1, TL).start()

        @pl.when(j + 1 < 8)
        def _():
            for cp in carry(j + 1, False):
                cp.start()
        ow[sl, 2] = lax.dot_general(dyt[...], hh[sl], NT, preferred_element_type=F32)
        slab0(j, TW).wait()
        out(j, TW).start()
        return 0
    lax.fori_loop(0, NW, step, 0)

    for cp in loads(NW, TL):
        cp.wait()
    sl = NW % 2
    for p in range(2):
        mr = pl.ds(p * (D // 2), D // 2)
        ow[sl, 1, mr, 0:TL] = lax.dot_general(xt[mr], db[sl, 0:TL], NT, preferred_element_type=F32)
        ow[sl, 2, mr, 0:TL] = lax.dot_general(dyt[mr], hh[sl, 0:TL], NT, preferred_element_type=F32)
    slab0(NW, TL).wait()
    out(NW, TL).start()
    out(NW - 1, TW).wait()
    out(NW, TL).wait()


def solution(mesh):
    def local_step(x_dev, dy_dev, gate_shard, up_shard, down_shard, g_dev):
        any_spec = pl.BlockSpec(memory_space=pl.ANY)
        sds = jax.ShapeDtypeStruct
        dma = pltpu.SemaphoreType.DMA
        vm = pltpu.VMEM
        outs = pl.pallas_call(
            step_kernel,
            in_specs=[any_spec] * 6,
            out_specs=[any_spec] * 13,
            out_shape=[sds((D, FF), F32), sds((N, D), BF16), sds((3, SH, D), F32),
                       sds((FF, D), BF16), sds((FF, D), BF16), sds((FF, D), BF16),
                       sds((UN, 2, UR, UC), BF16), sds((UN, UR, UC), BF16), sds((UN, UR, UC), BF16),
                       sds((FF, N), BF16), sds((FF, N), BF16), sds((D, N), BF16), sds((D, N), BF16)],
            scratch_shapes=[
                vm((D, N), BF16), vm((D, N), BF16), vm((D, N), F32),
                vm((3, 3 * FT, D), BF16), vm((3, D, 2 * FT), BF16), vm((2, D, FT), F32),
                vm((3 * FT, T), BF16), vm((3 * FT, T), BF16), vm((3 * FT, T), F32), vm((XS, XB, D), BF16),
                vm((2, UR, UC), F32), vm((2, UR, UC), F32), vm((3, 2, UR, UC), BF16),
                vm((2, UR, UC), BF16), vm((PS + 1, 2, UR, UC), BF16), vm((UR, UC), BF16),
                vm((QS + 1, UR, UC), BF16), vm((UR, UC), BF16), vm((3, UC, UR), F32),
                dma((3, 3)), dma((2,)), dma((XS,)), dma((2,)), dma((1,)), dma((3, 2)), dma((5, 3)), dma((5, 3)),
                dma((2,)), dma((2,)), dma((1,)), dma((1,)), dma((1,)), dma((2,)), dma((2, 2)), dma((2,)),
                dma((UN,)), dma((UN,)), dma((UN,)), dma((UN,)), dma((UN,)), dma((UN,)),
            ],
            compiler_params=pltpu.CompilerParams(collective_id=0, has_side_effects=True, vmem_limit_bytes=65470 * 1024),
        )(x_dev.reshape(N, D), dy_dev.reshape(N, D), gate_shard.T, up_shard.T, down_shard, g_dev[0])
        dw, dx, dn = pl.pallas_call(
            tail_kernel,
            in_specs=[any_spec] * 7,
            out_specs=[any_spec] * 3,
            out_shape=[sds((3, D, FF), F32), sds((N, D), BF16), sds((3, SH, D), F32)],
            scratch_shapes=[
                vm((D, N), BF16), vm((D, N), BF16), vm((2, TW, N), BF16), vm((2, TW, N), BF16), vm((2, 3, D, TW), F32),
                vm((2, N // 8, D), BF16), vm((2, 3, SH // 8, D), F32),
                dma((2,)), dma((2, 2)), dma((2,)), dma((2,)), dma((2, 2)), dma((2, 2)),
            ],
            compiler_params=pltpu.CompilerParams(vmem_limit_bytes=60 * 1024 * 1024),
        )(outs[11], outs[12], outs[9], outs[10], outs[0], outs[1], outs[2])
        return dx.reshape(2, N // 2, D), dn.transpose(0, 2, 1), dw[None]

    in_specs = (P(None, TOK_AXES, None), P(None, TOK_AXES, None), P(None, GROUP_AXES), P(None, GROUP_AXES), P(GROUP_AXES, None), P(TOK_AXES, None, None, None))
    out_specs = (P(None, TOK_AXES, None), P(None, None, GROUP_AXES), P(TOK_AXES, None, None, None))
    return jax.shard_map(local_step, mesh=mesh, in_specs=in_specs, out_specs=out_specs, check_vma=False)
```

time: 455 us -> 418 us (0.919)
  local copies, waits for them, and re-layouts: 50.9 us -> 0 us
  Pallas kernels: 403 us -> 417 us
    pallas_call x0 -> x1, Pallas kernels: none -> 85.5 us  [local_step(): pl.pallas_call(tail_kernel, in_specs=[any_spec] * 7, out_specs=[any_spec]...]
    pallas_call x1, Pallas kernels: 403 us -> 331 us  [local_step(): pl.pallas_call(step_kernel, in_specs=[any_spec] * 6, out_specs=[any_spec]...]
    unnamed x3 -> x0, local copies, waits for them, and re-layouts: 50.9 us -> none
where the time goes in v2:
time: 418 us; the launch traced here: 417 us
  Pallas kernels  417 us (100%)
    pallas_call x1, Pallas kernels, local_step(): pl.pallas_call(step_kernel, in_specs=[any_spec] * 6, out_specs=[any_spec]...  331 us
    pallas_call x1, Pallas kernels, local_step(): pl.pallas_call(tail_kernel, in_specs=[any_spec] * 7, out_specs=[any_spec]...  85.5 us

profile of v2, /device:TPU:0, one launch (start us, length us, event | category | flops | bytes accessed | tf_op | source)
XLA Modules:
  0.0 417.3 jit_solution(8318563978623933733)
XLA Ops:
  0.6 331.1 %shard_map.85 = (f32[896,4864]{1,0:T(8,128)}, bf16[4096,896]{1,0:T(8,128)(2,1)}, f32[3,1216,896]{2,1,0:T(8,128)}, bf16[4864,896]{1,0:T(8,128)(2,1)}, bf16[4864,8...) custom-call(bf16[4096,896]{1,0:T(8,128)(2,1)} %bitcast.9, ...), custom_call_target="tpu_custom_call" | custom-call | tf_op jit(solution)/shard_map/pallas_call | solution.py:616
  331.7 85.5 %shard_map.86 = (f32[3,896,4864]{2,1,0:T(8,128)}, bf16[4096,896]{1,0:T(8,128)(2,1)}, f32[3,1216,896]{2,1,0:T(8,128)}) custom-call(bf16[896,4096]{1,0:T(8,128)(2,1)} %get-tuple-element.13.xt_h, bf16[896,4096]{1,0:T(8,128)(2,1)} %get-tuple-element.14.dyt_h, bf16[4864,4096]{1,0:T(8,128)(2,1)} %get-tuple-element.15.db_h, ...), custom_call_target="tpu_custom_call" | custom-call | tf_op jit(solution)/shard_map/pallas_call | solution.py:637
